TPU v7x, 256 devices: a whole 4x4x8 slice. The times are simulated.
256 devices in a mesh: dp: 8 (over z_hi, core), comp: 32 (over x, z_lo, y).
Axes of the slice: x: 4, y: 4, z: 8 (z_hi: 4, z_lo: 2; z = z_hi * 2 + z_lo), core: 2. Of those that a mesh axis runs over, the one named last changes fastest.
Arguments:
- row_ids: int32 [8192], P('dp'), may hold values from 0 to 8191
- table: float32 [8192, 1024], P('comp'), may hold values from -25 to 25, as said below
- means: float32 [16384, 1024], P('comp'), may hold values from -0.3 to 0.3
- precisions: float32 [16384, 1024], P('comp'), may hold values from 0.8 to 1.2
- mix_logits: float32 [16384], P('comp'), may hold values from -2 to 2
- step_index: int32 [1], replicated, may hold values from 0 to 65535
Outputs:
- new_means: float32 [16384, 1024], P('comp')
- new_precisions: float32 [16384, 1024], P('comp')
- new_logits: float32 [16384], P('comp')
Inputs may be any that keep to these rules, and one draw needn't show every extreme that they name: `table`: embedding rows with entries of order one and row scales that differ.
All inputs are finite; a program needn't handle non-finite values.
Results may differ from a plain program's by a relative error of at most 0.0014.
Values sent between devices are 32-bit elements; how exact they have to be, the bound alone decides.
A program may use at most 64 MiB of HBM per device.

v0:
```python
import jax
import jax.numpy as jnp
from jax import lax
from jax.sharding import PartitionSpec as P


def split(value):
    high = lax.reduce_precision(value, 8, 7)
    return (high.astype(jnp.bfloat16), (value - high).astype(jnp.bfloat16))


def product(left, right, dims):

    def one(a, b):
        return lax.dot_general(a, b, (dims, ((), ())), preferred_element_type=jnp.float32)

    return one(left[0], right[0]) + (one(left[0], right[1]) + one(left[1], right[0]))


def multiplicity(ids, part, parts, owners, share):
    per_owner = parts * share
    owner = ids // per_owner
    within = ids % per_owner
    mine = within // share == part
    row = within % share
    left = (owner[None, :] == lax.broadcasted_iota(jnp.int32, (owners, 1), 0)) & mine[None, :]
    right = row[None, :] == lax.broadcasted_iota(jnp.int32, (share, 1), 0)
    found = lax.dot_general(
        left.astype(jnp.bfloat16),
        right.astype(jnp.bfloat16),
        (((1,), (1,)), ((), ())),
        preferred_element_type=jnp.float32,
    )
    return found.reshape(-1)


def local(row_ids, table, means, precisions, mix_logits, step_index):
    dp, comp = (lax.axis_size("dp"), lax.axis_size("comp"))
    part = lax.axis_index("dp")
    share = table.shape[0] // dp
    batch = 1.0 * row_ids.shape[0] * dp
    ids = lax.all_gather(row_ids, "dp", tiled=True)
    mine = lax.dynamic_slice_in_dim(table, part * share, share, 0)
    samples = lax.all_gather(mine, "comp", tiled=True)
    times = multiplicity(ids, part, dp, comp, share)
    squares = samples * samples
    s, q = (split(samples), split(squares))
    excess = precisions - 1.0
    cross = -2.0 * precisions * means
    e, c = (split(excess), split(cross))
    offset = (
        mix_logits
        + 0.5 * jnp.sum(jnp.log(precisions), axis=1)
        - 0.5 * jnp.sum(precisions * means * means, axis=1)
    )
    lanes = ((1,), (1,))
    quadratic = product(e, q, lanes) + product(c, s, lanes)
    scores = offset[:, None] - 0.5 * quadratic
    top = jnp.max(scores, axis=0)
    raised = jnp.exp(scores - top[None, :])
    mass = jnp.sum(raised, axis=0)
    logit_top = jnp.max(mix_logits)
    logit_raised = jnp.exp(mix_logits - logit_top)
    logit_mass = jnp.sum(logit_raised)
    packed = jnp.concatenate([top, mass, jnp.full((128,), logit_top), jnp.full((128,), logit_mass)])
    every = lax.all_gather(packed, "comp")
    rows = top.shape[0]
    tops, masses = (every[:, :rows], every[:, rows : 2 * rows])
    peak = jnp.max(tops, axis=0)
    total = jnp.sum(masses * jnp.exp(tops - peak[None, :]), axis=0)
    factor = jnp.exp(top - peak) / total * times
    resp = raised * factor[None, :]
    logit_tops, logit_masses = (every[:, 2 * rows], every[:, 2 * rows + 128])
    logit_peak = jnp.max(logit_tops)
    logit_total = jnp.sum(logit_masses * jnp.exp(logit_tops - logit_peak))
    weights = logit_raised * (jnp.exp(logit_top - logit_peak) / logit_total)
    counts = jnp.sum(resp, axis=1)
    r = split(resp)
    inner = ((1,), (0,))
    first = product(r, s, inner)
    second = product(r, q, inner)
    first, second = (
        lax.psum_scatter(x, "dp", scatter_dimension=0, tiled=True) for x in (first, second)
    )
    counts = lax.psum(counts, "dp")

    def own(x):
        size = x.shape[0] // dp
        return lax.dynamic_slice_in_dim(x, part * size, size, 0)

    step = (2.0 + step_index[0].astype(jnp.float32) / 8192.0) ** (-0.6)
    retain = 1.0 - step
    mass_all = retain * weights + step * counts / batch
    new_logits = jnp.log(mass_all)
    mass_new = own(mass_all)[:, None]
    prior = own(retain * weights)[:, None]
    own_counts = own(counts)[:, None]
    own_means = own(means)
    new_means = (prior * own_means + step * first / batch) / mass_new
    moved = own_means - new_means
    spread = (
        prior * (1.0 / own(precisions) + moved * moved)
        + step * (second - 2.0 * new_means * first + new_means * new_means * own_counts) / batch
    )
    new_precisions = mass_new / spread
    new_means, new_precisions = (
        lax.all_gather(x, "dp", tiled=True) for x in (new_means, new_precisions)
    )
    return (new_means, new_precisions, new_logits)


def solution(mesh):
    placed = (P("dp"), P("comp", None), P("comp", None), P("comp", None), P("comp"), P())
    return jax.shard_map(
        local,
        mesh=mesh,
        in_specs=placed,
        out_specs=(P("comp", None), P("comp", None), P("comp")),
        check_vma=False,
    )
```

profile of v0, /device:TPU:1, one launch (start us, length us, event | category | flops | bytes accessed | tf_op | source)
XLA Modules:
  0.0 447.8 jit_solution(17200917461490478965)
XLA Ops:
  9.1 19.7 %all_gather.21 = s32[8192]{0:T(1024)S(1)} all-gather(s32[1024]{0:T(1024)} %param.6), channel_id=1, replica_groups=mesh['dp'=8,'comp'=32] {'dp'}, dimensions={0}, use_global_device_ids=true | all-gather | bytes 36864 | tf_op jit(solution)/shard_map/all_gather | solution.py:42
  30.7 3.8 log_reduce_fusion
  35.7 118.0 %all-gather.6.cloned.1.call-done = f32[1024,1024]{1,0:T(8,128)} async-done(((f32[32,1024]{1,0:T(8,128)}), f32[1024,1024]{1,0:T(8,128)}) %all-gather.6.cloned.1.call-update) | async-done | bytes 4194320 | tf_op jit(solution)/shard_map/all_gather | solution.py:44
  153.7 2.9 reduce-precision_convert_fusion.1
  156.6 1.3 fusion.10
  158.0 1.3 fusion.27
  159.3 1.3 fusion.44
  161.5 1.3 fusion.18
  162.8 1.4 fusion.25
  165.0 1.7 fusion.43
  168.3 68.0 %all-gather.1 = f32[32,1,2304]{2,1,0:T(1,128)S(1)} all-gather(f32[1,1,2304]{2,1,0:T(1,128)S(1)} %reshape.45), channel_id=2, replica_groups=mesh['dp'=8,'comp'=32] {'comp'}, dimensions={0}, use_global_device_ids=true | all-gather | bytes 304128 | tf_op jit(solution)/shard_map/all_gather | solution.py:66
  238.1 1.3 fusion.16
  239.4 2.6 add_add_fusion.1
  242.2 3.3 fusion.46
  245.6 1.3 fusion.23
  247.2 2.6 add_add_fusion
  254.4 48.7 %psum.7 = f32[512]{0:T(512)S(1)} all-reduce(f32[512]{0:T(512)S(1)} %get-tuple-element.13), channel_id=1, replica_groups=mesh['dp'=8,'comp'=32] {'dp'}, use_global_device_ids=true, to_apply=%region_12.13 | all-reduce | flops 512 | bytes 4096 | tf_op jit(solution)/shard_map/psum | solution.py:85
  304.4 10.1 %reduce-scatter.3.cloned.1.call-done = f32[64,1024]{1,0:T(8,128)} async-done(((f32[512,1024]{1,0:T(8,128)}), f32[64,1024]{1,0:T(8,128)}) %reduce-scatter.3.cloned.1.call-update) | async-done | bytes 262160 | tf_op jit(solution)/shard_map/reduce_scatter | solution.py:83
  314.5 46.2 %reduce-scatter.5.cloned.1.call-done = f32[64,1024]{1,0:T(8,128)} async-done(((f32[512,1024]{1,0:T(8,128)}), f32[64,1024]{1,0:T(8,128)}) %reduce-scatter.5.cloned.1.call-update) | async-done | bytes 262160 | tf_op jit(solution)/shard_map/reduce_scatter | solution.py:83
  360.7 2.2 add_divide_fusion
  363.5 36.6 %all-gather.8.cloned.1.call-done = f32[512,1024]{1,0:T(8,128)} async-done(((f32[64,1024]{1,0:T(8,128)}), f32[512,1024]{1,0:T(8,128)}) %all-gather.8.cloned.1.call-update) | async-done | bytes 2097168 | tf_op jit(solution)/shard_map/all_gather | solution.py:107
  400.2 36.4 %all-gather.10.cloned.1.call-done = f32[512,1024]{1,0:T(8,128)} async-done(((f32[64,1024]{1,0:T(8,128)}), f32[512,1024]{1,0:T(8,128)}) %all-gather.10.cloned.1.call-update) | async-done | bytes 2097168 | tf_op jit(solution)/shard_map/all_gather | solution.py:107
  436.6 3.3 copy.15
  439.9 1.3 copy.16
  (60 shorter events, 14.4 us)
Async XLA Ops:
  7.2 1.2 copy-start
  7.2 146.5 %all-gather.6.cloned.1.call-start = ((), (), s32[]{:S(2)}) async-start(), calls=%async_computation.2 | async-start | bytes 4325376 | tf_op jit(solution)/shard_map/all_gather | solution.py:44
  9.1 305.4 %reduce-scatter.3.cloned.1.call-start = ((), (), s32[]{:S(2)}) async-start(), calls=%async_computation.3 | async-start | bytes 2359296 | tf_op jit(solution)/shard_map/reduce_scatter | solution.py:83
  30.7 3.8 copy-start.12
  35.7 120.9 %copy-start.1 = (f32[512,1024]{1,0:T(8,128)S(1)}, f32[512,1024]{1,0:T(8,128)}, u32[]{:S(2)}) copy-start(f32[512,1024]{1,0:T(8,128)} %param.9) | copy-start | bytes 6291460
  156.6 1.3 copy-start.7
  157.9 1.3 copy-start.11
  159.3 2.2 copy-start.4
  162.8 1.6 copy-start.2
  162.8 2.2 copy-start.3
  236.9 1.3 copy-start.9
  242.1 118.6 %reduce-scatter.5.cloned.1.call-start = ((), (), s32[]{:S(2)}) async-start(), calls=%async_computation.5 | async-start | bytes 2359296 | tf_op jit(solution)/shard_map/reduce_scatter | solution.py:83
  242.1 3.3 copy-start.5
  242.1 3.4 copy-start.10
  245.6 1.6 copy-start.8
  249.8 150.4 %all-gather.8.cloned.1.call-start = ((), (), s32[]{:S(2)}) async-start(), calls=%async_computation.4 | async-start | bytes 2359296 | tf_op jit(solution)/shard_map/all_gather | solution.py:107
  362.9 73.6 %all-gather.10.cloned.1.call-start = ((), (), s32[]{:S(2)}) async-start(), calls=%async_computation.6 | async-start | bytes 2359296 | tf_op jit(solution)/shard_map/all_gather | solution.py:107
  436.6 3.3 copy-start.6
Sparse Core Ops, SparseCore 0:
  10.4 143.2 all-gather.5
  242.2 72.2 reduce-scatter.2
  317.6 43.0 reduce-scatter.4
  363.1 37.0 all-gather.7
  402.5 34.0 all-gather.9
where the time goes:
time: 448 us
  waiting for transfers between devices  248 us (55%)
  blocking collectives  136 us (30%)
  matrix products  21.1 us (5%)
  between operations  16.7 us (4%)
  other arithmetic  15.3 us (3%)
  local copies, waits for them, and re-layouts  10.1 us (2%)
    all_gather x1, waiting for transfers between devices, local(): samples = lax.all_gather(mine, 'comp', tiled=True)  118 us
    all_gather x2, waiting for transfers between devices, local(): lax.all_gather(x, 'dp', tiled=True)  73.1 us
    all_gather x1, blocking collectives, local(): every = lax.all_gather(packed, 'comp')  68 us
    reduce_scatter x2, waiting for transfers between devices, local(): lax.psum_scatter(x, 'dp', scatter_dimension=0, tiled=True)  56.3 us
    psum x1, blocking collectives, local(): counts = lax.psum(counts, 'dp')  48.7 us
    dot_general x12, matrix products, one(): lax.dot_general(a, b, (dims, ((), ())), preferred_element_type=jnp.float32)  20.6 us
    all_gather x1, blocking collectives, local(): ids = lax.all_gather(row_ids, 'dp', tiled=True)  19.7 us
  transfers between devices with their start and end apart: 5, of which 5 were waited for; matrix products, arithmetic and copies ran while one was open for 4% of the time, Pallas kernels for 0%

commit v1 on v0

--- a/solution.py
+++ b/solution.py
@@ -41,7 +41,9 @@
     batch = 1.0 * row_ids.shape[0] * dp
     ids = lax.all_gather(row_ids, "dp", tiled=True)
     mine = lax.dynamic_slice_in_dim(table, part * share, share, 0)
-    samples = lax.all_gather(mine, "comp", tiled=True)
+    samples = jnp.concatenate(
+        lax.all_to_all(jnp.stack([mine] * lax.axis_size("comp")), "comp", 0, 0), axis=0
+    )
     times = multiplicity(ids, part, dp, comp, share)
     squares = samples * samples
     s, q = (split(samples), split(squares))

time: 448 us -> 363 us (0.81)
  waiting for transfers between devices: 248 us -> 129 us
  blocking collectives: 136 us -> 160 us
  starting transfers between devices: 0.21 us -> 9.65 us
    all_gather x1 -> x0, waiting for transfers between devices: 118 us -> none  [local(): samples = lax.all_gather(mine, 'comp', tiled=True)]
    all_gather x1, blocking collectives: 19.7 us -> 65.8 us  [local(): ids = lax.all_gather(row_ids, 'dp', tiled=True)]
    psum x1, blocking collectives: 48.7 us -> 28.2 us  [local(): counts = lax.psum(counts, 'dp')]
    all_to_all x0 -> x1, starting transfers between devices: none -> 9.48 us  [local(): lax.all_to_all(jnp.stack([mine] * lax.axis_size('comp')), 'comp', 0, 0)]
  transfers between devices with their start and end apart: 5 -> 5, of which waited for: 5 -> 4; matrix products, arithmetic and copies ran while one was open for 4% -> 4% of each run, Pallas kernels for 0% -> 0%
where the time goes in v1:
time: 363 us
  blocking collectives  160 us (44%)
  waiting for transfers between devices  129 us (36%)
  matrix products  21.1 us (6%)
  between operations  16.7 us (5%)
  other arithmetic  15.4 us (4%)
  local copies, waits for them, and re-layouts  10.9 us (3%)
  starting transfers between devices  9.65 us (3%)
    all_gather x2, waiting for transfers between devices, local(): lax.all_gather(x, 'dp', tiled=True)  73.5 us
    all_gather x1, blocking collectives, local(): every = lax.all_gather(packed, 'comp')  66.5 us
    all_gather x1, blocking collectives, local(): ids = lax.all_gather(row_ids, 'dp', tiled=True)  65.8 us
    reduce_scatter x2, waiting for transfers between devices, local(): lax.psum_scatter(x, 'dp', scatter_dimension=0, tiled=True)  54.7 us
    psum x1, blocking collectives, local(): counts = lax.psum(counts, 'dp')  28.2 us
    dot_general x12, matrix products, one(): lax.dot_general(a, b, (dims, ((), ())), preferred_element_type=jnp.float32)  20.6 us
    all_to_all x1, starting transfers between devices, local(): lax.all_to_all(jnp.stack([mine] * lax.axis_size('comp')), 'comp', 0, 0)  9.48 us
  transfers between devices with their start and end apart: 5, of which 4 were waited for; matrix products, arithmetic and copies ran while one was open for 4% of the time, Pallas kernels for 0%

profile of v1, /device:TPU:1, one launch (start us, length us, event | category | flops | bytes accessed | tf_op | source)
XLA Modules:
  0.0 362.9 jit_solution(6510420617838256857)
XLA Ops:
  8.4 2.5 stack.2
  10.9 9.5 %all-to-all-start = ((f32[32,32,1024]{2,1,0:T(8,128)}), f32[32,32,1024]{2,1,0:T(8,128)}, u32[]{:S(2)}, u32[]{:S(2)}) async-start(f32[32,32,1024]{2,1,0:T(8,128)} %stack.2), calls=%async_computation | async-start | bytes 8388608 | tf_op jit(solution)/shard_map/all_to_all | solution.py:45
  20.5 65.8 %all_gather.17 = s32[8192]{0:T(1024)S(1)} all-gather(s32[1024]{0:T(1024)S(1)} %copy-done.12), channel_id=1, replica_groups=mesh['dp'=8,'comp'=32] {'dp'}, dimensions={0}, use_global_device_ids=true | all-gather | bytes 36864 | tf_op jit(solution)/shard_map/all_gather | solution.py:42
  87.5 3.3 log_reduce_fusion
  92.1 3.9 %fusion = (bf16[1024,1024]{1,0:T(8,128)(2,1)S(1)}, bf16[1024,1024]{1,0:T(8,128)(2,1)S(1)}, bf16[1024,1024]{1,0:T(8,128)(2,1)S(1)}, bf16[1024,1024]{1,0:T(8,128)(2,1)S(1)}) fusion(f32[32,32,1024]{2,1,0:T(8,128)} %all-to-all-done), kind=kLoop, calls=%fused_computation.4 | loop fusion | flops 9437184 | bytes 12582912 | tf_op jit(solution)/shard_map/convert_element_type | solution.py:9
  96.0 1.3 fusion.10
  97.3 1.3 fusion.20
  98.6 1.3 fusion.37
  99.9 1.3 fusion.38
  101.2 1.3 fusion.19
  103.5 1.8 fusion.36
  106.9 66.5 %all-gather.1 = f32[32,1,2304]{2,1,0:T(1,128)S(1)} all-gather(f32[1,1,2304]{2,1,0:T(1,128)S(1)} %reshape.51), channel_id=2, replica_groups=mesh['dp'=8,'comp'=32] {'comp'}, dimensions={0}, use_global_device_ids=true | all-gather | bytes 304128 | tf_op jit(solution)/shard_map/all_gather | solution.py:68
  176.5 2.7 add_add_fusion.1
  179.3 3.3 fusion.42
  182.6 1.3 fusion.41
  183.9 2.6 add_add_fusion
  191.2 28.2 %psum.7 = f32[512]{0:T(512)S(1)} all-reduce(f32[512]{0:T(512)S(1)} %get-tuple-element.15), channel_id=1, replica_groups=mesh['dp'=8,'comp'=32] {'dp'}, use_global_device_ids=true, to_apply=%region_12.13 | all-reduce | flops 512 | bytes 4096 | tf_op jit(solution)/shard_map/psum | solution.py:87
  220.8 8.3 %reduce-scatter.3.cloned.1.call-done = f32[64,1024]{1,0:T(8,128)} async-done(((f32[512,1024]{1,0:T(8,128)}), f32[64,1024]{1,0:T(8,128)}) %reduce-scatter.3.cloned.1.call-update) | async-done | bytes 262160 | tf_op jit(solution)/shard_map/reduce_scatter | solution.py:85
  229.1 46.3 %reduce-scatter.5.cloned.1.call-done = f32[64,1024]{1,0:T(8,128)} async-done(((f32[512,1024]{1,0:T(8,128)}), f32[64,1024]{1,0:T(8,128)}) %reduce-scatter.5.cloned.1.call-update) | async-done | bytes 262160 | tf_op jit(solution)/shard_map/reduce_scatter | solution.py:85
  275.4 2.2 add_divide_fusion
  278.3 37.1 %all-gather.5.cloned.1.call-done = f32[512,1024]{1,0:T(8,128)} async-done(((f32[64,1024]{1,0:T(8,128)}), f32[512,1024]{1,0:T(8,128)}) %all-gather.5.cloned.1.call-update) | async-done | bytes 2097168 | tf_op jit(solution)/shard_map/all_gather | solution.py:109
  315.4 36.4 %all-gather.7.cloned.1.call-done = f32[512,1024]{1,0:T(8,128)} async-done(((f32[64,1024]{1,0:T(8,128)}), f32[512,1024]{1,0:T(8,128)}) %all-gather.7.cloned.1.call-update) | async-done | bytes 2097168 | tf_op jit(solution)/shard_map/all_gather | solution.py:109
  351.8 3.3 copy.15
  355.1 1.3 copy.16
  (60 shorter events, 13.4 us)
Async XLA Ops:
  7.2 1.2 copy-start
  10.9 9.5 %copy-start.12 = (s32[1024]{0:T(1024)S(1)}, s32[1024]{0:T(1024)}, u32[]{:S(2)}) copy-start(s32[1024]{0:T(1024)} %param.6) | copy-start | bytes 12292
  10.9 76.0 %copy-start.11 = (f32[512]{0:T(512)S(1)}, f32[512]{0:T(512)}, u32[]{:S(2)}) copy-start(f32[512]{0:T(512)} %param.10) | copy-start | bytes 6148
  10.9 76.6 %copy-start.1 = (f32[512,1024]{1,0:T(8,128)S(1)}, f32[512,1024]{1,0:T(8,128)}, u32[]{:S(2)}) copy-start(f32[512,1024]{1,0:T(8,128)} %param.9) | copy-start | bytes 6291460
  10.9 81.1 %all-to-all-start = ((f32[32,32,1024]{2,1,0:T(8,128)}), f32[32,32,1024]{2,1,0:T(8,128)}, u32[]{:S(2)}, u32[]{:S(2)}) async-start(f32[32,32,1024]{2,1,0:T(8,128)} %stack.2), calls=%async_computation | async-start | bytes 8388608 | tf_op jit(solution)/shard_map/all_to_all | solution.py:45
  20.4 208.7 %reduce-scatter.3.cloned.1.call-start = ((), (), s32[]{:S(2)}) async-start(), calls=%async_computation.3 | async-start | bytes 2359296 | tf_op jit(solution)/shard_map/reduce_scatter | solution.py:85
  96.0 1.3 copy-start.5
  96.0 5.2 %copy-start.7 = (bf16[1024,1024]{1,0:T(8,128)(2,1)}, bf16[1024,1024]{1,0:T(8,128)(2,1)S(1)}, u32[]{:S(2)}) copy-start(bf16[1024,1024]{1,0:T(8,128)(2,1)S(1)} %get-tuple-element.9) | copy-start | bytes 6291460
  97.3 1.3 copy-start.10
  101.2 1.6 copy-start.2
  101.2 2.2 copy-start.3
  174.0 1.3 copy-start.8
  179.2 96.2 %reduce-scatter.5.cloned.1.call-start = ((), (), s32[]{:S(2)}) async-start(), calls=%async_computation.5 | async-start | bytes 2359296 | tf_op jit(solution)/shard_map/reduce_scatter | solution.py:85
  179.2 3.3 copy-start.6
  179.3 3.3 copy-start.9
  186.5 128.8 %all-gather.5.cloned.1.call-start = ((), (), s32[]{:S(2)}) async-start(), calls=%async_computation.4 | async-start | bytes 2359296 | tf_op jit(solution)/shard_map/all_gather | solution.py:109
  277.7 74.1 %all-gather.7.cloned.1.call-start = ((), (), s32[]{:S(2)}) async-start(), calls=%async_computation.6 | async-start | bytes 2359296 | tf_op jit(solution)/shard_map/all_gather | solution.py:109
  351.8 3.3 copy-start.4
Sparse Core Ops, SparseCore 0:
  179.3 49.7 reduce-scatter.2
  232.2 43.1 reduce-scatter.4
  277.9 37.4 all-gather.4
  317.6 34.0 all-gather.6
